TPU v7x, 32 devices: a whole 2x2x4 slice. The times are simulated.
32 devices in a mesh: section: 4 (over z), dom: 8 (over y, x, core).
Axes of the slice: x: 2, y: 2, z: 4, core: 2. Of those that a mesh axis runs over, the one named last changes fastest.
Arguments:
- layer_inputs: bfloat16 [4, 16384, 512], P('section', 'dom'), may hold values from -6 to 6
- adjacency: bfloat16 [128, 8, 128, 128], P('dom'), may hold values from -0.1875 to 0.1875
- columns: int32 [128, 8], P('dom'), may hold values from 0 to 127, as said below
- group_order: int32 [8, 4], P('dom'), may hold values from 0 to 3, each once within a row
- weights: bfloat16 [4, 512, 512], P('section'), may hold values from -0.25 to 0.25
Outputs:
- embeddings: bfloat16 [4, 16384, 512], P('section', 'dom')
Inputs may be any that keep to these rules, and one draw needn't show every extreme that they name: `columns`: the tiles of a row block of part p name row blocks of parts p - 1, p and p + 1, counted modulo 8. `group_order`: each row is a permutation.
All inputs are finite; a program needn't handle non-finite values.
Results may differ from a plain program's by a relative error of at most 0.0095.
Values may be sent and summed in bfloat16 or wider, within the bound.
A program may use at most 64 MiB of HBM per device.

v0:
```python
import jax
import jax.numpy as jnp
from jax import lax
from jax.sharding import PartitionSpec as P


def with_halo(x, sides, width):
    for axis, dim in sides:
        devices, length = (lax.axis_size(axis), x.shape[dim])
        up = [(i, (i + 1) % devices) for i in range(devices)]
        down = [(j, i) for i, j in up]
        last = lax.slice_in_dim(x, length - width, length, axis=dim)
        leading = lax.slice_in_dim(x, 0, width, axis=dim)
        before = lax.ppermute(last, axis, up)
        after = lax.ppermute(leading, axis, down)
        x = jnp.concatenate([before, x, after], axis=dim)
    return x


def passed_along(x, axis, by):
    devices = lax.axis_size(axis)
    pairs = [(i, i + by) for i in range(devices) if 0 <= i + by < devices]
    return lax.ppermute(x, axis, pairs)


def on_device(layer_inputs, adjacency, columns, group_order, weights):
    part_count = lax.axis_size("dom")
    my_part = lax.axis_index("dom")
    my_section = lax.axis_index("section")
    stale_rows = layer_inputs[0]
    node_rows, width = stale_rows.shape
    group_count = group_order.shape[1]
    span = node_rows // group_count
    blocks_part = adjacency.shape[0]
    blocks_group = blocks_part // group_count
    block_side = adjacency.shape[2]
    weight = weights[0]
    orders = with_halo(group_order, (("dom", 0),), 1)
    buffer_start = with_halo(stale_rows, (("dom", 0),), node_rows)
    relative = (columns // blocks_part - my_part + 1) % part_count
    local_index = relative * blocks_part + columns % blocks_part
    step_count = group_count + lax.axis_size("section") - 1

    def compute(own_group, group_in, buffer):
        tile_group = lax.dynamic_slice_in_dim(adjacency, own_group * blocks_group, blocks_group, 0)
        index_group = lax.dynamic_slice_in_dim(
            local_index, own_group * blocks_group, blocks_group, 0
        )
        sources = buffer.reshape(3 * blocks_part, block_side, width)[index_group]
        summed = jnp.einsum(
            "rkij,rkjd->rid", tile_group, sources, preferred_element_type=jnp.float32
        )
        aggregate = summed.astype(jnp.bfloat16).reshape(span, width)
        product = jnp.dot(aggregate, weight, preferred_element_type=jnp.float32)
        return (group_in.astype(jnp.float32) + jax.nn.relu(product)).astype(jnp.bfloat16)

    def place(target, piece, offset, active):
        previous = lax.dynamic_slice_in_dim(target, offset, span, 0)
        return lax.dynamic_update_slice_in_dim(
            target, jnp.where(active, piece, previous), offset, 0
        )

    def advance(step_index, carry):
        outgoing, buffer, hidden = carry
        position = step_index - my_section
        active = (position >= 0) & (position < group_count)
        position = jnp.clip(position, 0, group_count - 1)
        group_before = orders[0, position]
        group_own = orders[1, position]
        group_after = orders[2, position]
        arrived = passed_along(outgoing, "section", 1)
        own_stored = lax.dynamic_slice_in_dim(stale_rows, group_own * span, span, 0)
        group_in = jnp.where(my_section == 0, own_stored, arrived)
        widened = with_halo(group_in, (("dom", 0),), span)
        buffer = place(buffer, widened[:span], group_before * span, active)
        buffer = place(buffer, widened[span : 2 * span], node_rows + group_own * span, active)
        buffer = place(buffer, widened[2 * span :], 2 * node_rows + group_after * span, active)
        result = compute(group_own, group_in, buffer)
        hidden = place(hidden, result, group_own * span, active)
        outgoing = result
        return (outgoing, buffer, hidden)

    outgoing_start = jnp.zeros((span, width), jnp.bfloat16)
    hidden_start = jnp.zeros((node_rows, width), jnp.bfloat16)
    final_carry = lax.fori_loop(
        0, step_count, advance, (outgoing_start, buffer_start, hidden_start)
    )
    return final_carry[2][None]


def solution(mesh):
    in_specs = (
        P("section", "dom", None),
        P("dom", None, None, None),
        P("dom", None),
        P("dom", None),
        P("section", None, None),
    )
    out_specs = P("section", "dom", None)
    return jax.shard_map(
        on_device, mesh=mesh, in_specs=in_specs, out_specs=out_specs, check_vma=False
    )
```

profile of v0, /device:TPU:27, one launch (start us, length us, event | category | flops | bytes accessed | tf_op | source)
XLA Modules:
  0.0 369.0 jit_solution(3685461861889727582)
XLA Ops:
  3.9 42.7 %collective-permute-done.5 = s32[1,4]{1,0:T(1,128)S(1)} collective-permute-done((s32[1,4]{1,0:T(1,128)}, s32[1,4]{1,0:T(1,128)S(1)}, u32[]{:S(2)}, u32[]{:S(2)}) %collective-permute-start.5) | collective-permute-done | bytes 48 | tf_op jit(solution)/shard_map/ppermute | solution.py:14
  49.8 5.5 %pad_maximum_fusion = bf16[6144,512]{1,0:T(8,128)(2,1)} fusion(bf16[2048,512]{1,0:T(8,128)(2,1)S(1)} %collective-permute-done.4, bf16[2048,512]{1,0:T(8,128)(2,1)} %bitcast.48, bf16[2048,512]{1,0:T(8,128)(2,1)} %collective-permute-done.3), kind=kLoop, calls=%fused_computation.19 | loop fusion | flops 18874368 | bytes 12582912 | tf_op jit(solution)/shard_map/concatenate | solution.py:16
  56.8 312.3 %while.20 = (s32[]{:T(128)}, bf16[512,512]{1,0:T(8,128)(2,1)S(1)}, bf16[6144,512]{1,0:T(8,128)(2,1)}, bf16[2048,512]{1,0:T(8,128)(2,1)}, pred[]{:T(512)}, /*inde...) while((s32[]{:T(128)}, bf16[512,512]{1,0:T(8,128)(2,1)S(1)}, ...), condition=%wide.region_1.2_spmd.clone, body=%wide.region_0.1_spmd.clone.sunk | while | flops 808191104 | bytes 30938536 | solution.py:85
  59.5 12.2 %collective-permute-done = bf16[512,512]{1,0:T(8,128)(2,1)S(1)} collective-permute-done((bf16[512,512]{1,0:T(8,128)(2,1)S(1)}, bf16[512,512]{1,0:T(8,128)(2,1)S(1)}, u32[]{:S(2)}, u32[]{:S(2)}) %collective-permute-start) | collective-permute-done | bytes 524320 | tf_op jit(solution)/shard_map/while/body/eval_jaxpr/ppermute | solution.py:23
  75.9 7.8 %collective-permute-done.1 = bf16[512,512]{1,0:T(8,128)(2,1)S(1)} collective-permute-done((bf16[512,512]{1,0:T(8,128)(2,1)S(1)}, bf16[512,512]{1,0:T(8,128)(2,1)S(1)}, u32[]{:S(2)}, u32[]{:S(2)}) %collective-permute-start.1) | collective-permute-done | bytes 524320 | tf_op jit(solution)/shard_map/while/body/eval_jaxpr/ppermute | solution.py:14
  89.8 5.6 %gather_fusion = bf16[32,128,512]{2,1,0:T(8,128)(2,1)} fusion(bf16[48,128,512]{2,1,0:T(8,128)(2,1)} %bitcast.44, s32[1024]{0:T(1024)S(1)} %pad_clamp_fusion.2), kind=kCustom, calls=%fused_computation.clone.clone.1 | custom fusion | bytes 8388736 | tf_op jit(solution)/shard_map/while/body/eval_jaxpr/gather | solution.py:49
  103.8 11.0 %collective-permute-done = bf16[512,512]{1,0:T(8,128)(2,1)S(1)} collective-permute-done((bf16[512,512]{1,0:T(8,128)(2,1)S(1)}, bf16[512,512]{1,0:T(8,128)(2,1)S(1)}, u32[]{:S(2)}, u32[]{:S(2)}) %collective-permute-start) | collective-permute-done | bytes 524320 | tf_op jit(solution)/shard_map/while/body/eval_jaxpr/ppermute | solution.py:23
  122.1 8.4 %collective-permute-done.1 = bf16[512,512]{1,0:T(8,128)(2,1)S(1)} collective-permute-done((bf16[512,512]{1,0:T(8,128)(2,1)S(1)}, bf16[512,512]{1,0:T(8,128)(2,1)S(1)}, u32[]{:S(2)}, u32[]{:S(2)}) %collective-permute-start.1) | collective-permute-done | bytes 524320 | tf_op jit(solution)/shard_map/while/body/eval_jaxpr/ppermute | solution.py:14
  136.5 5.6 %gather_fusion = bf16[32,128,512]{2,1,0:T(8,128)(2,1)} fusion(bf16[48,128,512]{2,1,0:T(8,128)(2,1)} %bitcast.44, s32[1024]{0:T(1024)S(1)} %pad_clamp_fusion.2), kind=kCustom, calls=%fused_computation.clone.clone.1 | custom fusion | bytes 8388736 | tf_op jit(solution)/shard_map/while/body/eval_jaxpr/gather | solution.py:49
  150.4 11.9 %collective-permute-done = bf16[512,512]{1,0:T(8,128)(2,1)S(1)} collective-permute-done((bf16[512,512]{1,0:T(8,128)(2,1)S(1)}, bf16[512,512]{1,0:T(8,128)(2,1)S(1)}, u32[]{:S(2)}, u32[]{:S(2)}) %collective-permute-start) | collective-permute-done | bytes 524320 | tf_op jit(solution)/shard_map/while/body/eval_jaxpr/ppermute | solution.py:23
  177.8 5.6 %gather_fusion = bf16[32,128,512]{2,1,0:T(8,128)(2,1)} fusion(bf16[48,128,512]{2,1,0:T(8,128)(2,1)} %bitcast.44, s32[1024]{0:T(1024)S(1)} %pad_clamp_fusion.2), kind=kCustom, calls=%fused_computation.clone.clone.1 | custom fusion | bytes 8388736 | tf_op jit(solution)/shard_map/while/body/eval_jaxpr/gather | solution.py:49
  191.7 7.2 %collective-permute-done = bf16[512,512]{1,0:T(8,128)(2,1)S(1)} collective-permute-done((bf16[512,512]{1,0:T(8,128)(2,1)S(1)}, bf16[512,512]{1,0:T(8,128)(2,1)S(1)}, u32[]{:S(2)}, u32[]{:S(2)}) %collective-permute-start) | collective-permute-done | bytes 524320 | tf_op jit(solution)/shard_map/while/body/eval_jaxpr/ppermute | solution.py:23
  200.2 8.5 %collective-permute-start.1 = (bf16[512,512]{1,0:T(8,128)(2,1)S(1)}, bf16[512,512]{1,0:T(8,128)(2,1)S(1)}, u32[]{:S(2)}, u32[]{:S(2)}) collective-permute-start(bf16[512,512]{1,0:T(8,128)(2,1)S(1)} %dynamic-slice_select_fusion.2), channel_id=1, source_target_pairs={{0,1},{1,2},{2,3},{3,4},{4,5},{5,6},{6,7},{7,0},{8,9},{9,10},{10,1... | collective-permute-start | bytes 1572872 | tf_op jit(solution)/shard_map/while/body/eval_jaxpr/ppermute | solution.py:14
  210.7 8.5 %collective-permute-done.1 = bf16[512,512]{1,0:T(8,128)(2,1)S(1)} collective-permute-done((bf16[512,512]{1,0:T(8,128)(2,1)S(1)}, bf16[512,512]{1,0:T(8,128)(2,1)S(1)}, u32[]{:S(2)}, u32[]{:S(2)}) %collective-permute-start.1) | collective-permute-done | bytes 524320 | tf_op jit(solution)/shard_map/while/body/eval_jaxpr/ppermute | solution.py:14
  225.2 5.6 %gather_fusion = bf16[32,128,512]{2,1,0:T(8,128)(2,1)} fusion(bf16[48,128,512]{2,1,0:T(8,128)(2,1)} %bitcast.44, s32[1024]{0:T(1024)S(1)} %pad_clamp_fusion.2), kind=kCustom, calls=%fused_computation.clone.clone.1 | custom fusion | bytes 8388736 | tf_op jit(solution)/shard_map/while/body/eval_jaxpr/gather | solution.py:49
  239.1 10.9 %collective-permute-done = bf16[512,512]{1,0:T(8,128)(2,1)S(1)} collective-permute-done((bf16[512,512]{1,0:T(8,128)(2,1)S(1)}, bf16[512,512]{1,0:T(8,128)(2,1)S(1)}, u32[]{:S(2)}, u32[]{:S(2)}) %collective-permute-start) | collective-permute-done | bytes 524320 | tf_op jit(solution)/shard_map/while/body/eval_jaxpr/ppermute | solution.py:23
  254.2 9.0 %collective-permute-done.1 = bf16[512,512]{1,0:T(8,128)(2,1)S(1)} collective-permute-done((bf16[512,512]{1,0:T(8,128)(2,1)S(1)}, bf16[512,512]{1,0:T(8,128)(2,1)S(1)}, u32[]{:S(2)}, u32[]{:S(2)}) %collective-permute-start.1) | collective-permute-done | bytes 524320 | tf_op jit(solution)/shard_map/while/body/eval_jaxpr/ppermute | solution.py:14
  269.1 5.6 %gather_fusion = bf16[32,128,512]{2,1,0:T(8,128)(2,1)} fusion(bf16[48,128,512]{2,1,0:T(8,128)(2,1)} %bitcast.44, s32[1024]{0:T(1024)S(1)} %pad_clamp_fusion.2), kind=kCustom, calls=%fused_computation.clone.clone.1 | custom fusion | bytes 8388736 | tf_op jit(solution)/shard_map/while/body/eval_jaxpr/gather | solution.py:49
  283.0 10.4 %collective-permute-done = bf16[512,512]{1,0:T(8,128)(2,1)S(1)} collective-permute-done((bf16[512,512]{1,0:T(8,128)(2,1)S(1)}, bf16[512,512]{1,0:T(8,128)(2,1)S(1)}, u32[]{:S(2)}, u32[]{:S(2)}) %collective-permute-start) | collective-permute-done | bytes 524320 | tf_op jit(solution)/shard_map/while/body/eval_jaxpr/ppermute | solution.py:23
  298.1 9.5 %collective-permute-done.1 = bf16[512,512]{1,0:T(8,128)(2,1)S(1)} collective-permute-done((bf16[512,512]{1,0:T(8,128)(2,1)S(1)}, bf16[512,512]{1,0:T(8,128)(2,1)S(1)}, u32[]{:S(2)}, u32[]{:S(2)}) %collective-permute-start.1) | collective-permute-done | bytes 524320 | tf_op jit(solution)/shard_map/while/body/eval_jaxpr/ppermute | solution.py:14
  313.5 5.6 %gather_fusion = bf16[32,128,512]{2,1,0:T(8,128)(2,1)} fusion(bf16[48,128,512]{2,1,0:T(8,128)(2,1)} %bitcast.44, s32[1024]{0:T(1024)S(1)} %pad_clamp_fusion.2), kind=kCustom, calls=%fused_computation.clone.clone.1 | custom fusion | bytes 8388736 | tf_op jit(solution)/shard_map/while/body/eval_jaxpr/gather | solution.py:49
  327.5 9.9 %collective-permute-done = bf16[512,512]{1,0:T(8,128)(2,1)S(1)} collective-permute-done((bf16[512,512]{1,0:T(8,128)(2,1)S(1)}, bf16[512,512]{1,0:T(8,128)(2,1)S(1)}, u32[]{:S(2)}, u32[]{:S(2)}) %collective-permute-start) | collective-permute-done | bytes 524320 | tf_op jit(solution)/shard_map/while/body/eval_jaxpr/ppermute | solution.py:23
  342.6 9.3 %collective-permute-done.1 = bf16[512,512]{1,0:T(8,128)(2,1)S(1)} collective-permute-done((bf16[512,512]{1,0:T(8,128)(2,1)S(1)}, bf16[512,512]{1,0:T(8,128)(2,1)S(1)}, u32[]{:S(2)}, u32[]{:S(2)}) %collective-permute-start.1) | collective-permute-done | bytes 524320 | tf_op jit(solution)/shard_map/while/body/eval_jaxpr/ppermute | solution.py:14
  357.8 5.6 %gather_fusion = bf16[32,128,512]{2,1,0:T(8,128)(2,1)} fusion(bf16[48,128,512]{2,1,0:T(8,128)(2,1)} %bitcast.44, s32[1024]{0:T(1024)S(1)} %pad_clamp_fusion.2), kind=kCustom, calls=%fused_computation.clone.clone.1 | custom fusion | bytes 8388736 | tf_op jit(solution)/shard_map/while/body/eval_jaxpr/gather | solution.py:49
  (119 shorter events, 127.7 us)
Async XLA Ops:
  0.0 49.8 %collective-permute-start.4 = (bf16[2048,512]{1,0:T(8,128)(2,1)}, bf16[2048,512]{1,0:T(8,128)(2,1)S(1)}, u32[]{:S(2)}, u32[]{:S(2)}) collective-permute-start(bf16[2048,512]{1,0:T(8,128)(2,1)} %bitcast.46), channel_id=1, source_target_pairs={{1,0},{2,1},{3,2},{4,3},{5,4},{6,5},{7,6},{0,7},{9,8},{10,9},{11,1... | collective-permute-start | bytes 6291464 | tf_op jit(solution)/shard_map/ppermute | solution.py:15
  0.7 49.1 %collective-permute-start.3 = (bf16[2048,512]{1,0:T(8,128)(2,1)}, bf16[2048,512]{1,0:T(8,128)(2,1)}, u32[]{:S(2)}, u32[]{:S(2)}) collective-permute-start(bf16[2048,512]{1,0:T(8,128)(2,1)} %bitcast.47), channel_id=1, source_target_pairs={{0,1},{1,2},{2,3},{3,4},{4,5},{5,6},{6,7},{7,0},{8,9},{9,10},{10,1... | collective-permute-start | bytes 6291464 | tf_op jit(solution)/shard_map/ppermute | solution.py:14
  2.6 44.0 %collective-permute-start.5 = (s32[1,4]{1,0:T(1,128)}, s32[1,4]{1,0:T(1,128)S(1)}, u32[]{:S(2)}, u32[]{:S(2)}) collective-permute-start(s32[1,4]{1,0:T(1,128)} %param.10), channel_id=1, source_target_pairs={{0,1},{1,2},{2,3},{3,4},{4,5},{5,6},{6,7},{7,0},{8,9},{9,10},{10,1... | collective-permute-start | bytes 56 | tf_op jit(solution)/shard_map/ppermute | solution.py:14
  2.7 46.4 %collective-permute-start.6 = (s32[1,4]{1,0:T(1,128)}, s32[1,4]{1,0:T(1,128)S(1)}, u32[]{:S(2)}, u32[]{:S(2)}) collective-permute-start(s32[1,4]{1,0:T(1,128)} %param.10), channel_id=1, source_target_pairs={{1,0},{2,1},{3,2},{4,3},{5,4},{6,5},{7,6},{0,7},{9,8},{10,9},{11,1... | collective-permute-start | bytes 56 | tf_op jit(solution)/shard_map/ppermute | solution.py:15
  56.8 14.9 %collective-permute-start = (bf16[512,512]{1,0:T(8,128)(2,1)S(1)}, bf16[512,512]{1,0:T(8,128)(2,1)S(1)}, u32[]{:S(2)}, u32[]{:S(2)}) collective-permute-start(bf16[512,512]{1,0:T(8,128)(2,1)S(1)} %broadcast_select_fusion.2), channel_id=1, source_target_pairs={{0,8},{8,16},{16,24},{1,9},{9,17},{17,25},{2,10},{10,18},{18,26},{... | collective-permute-start | bytes 1572872 | tf_op jit(solution)/shard_map/while/body/eval_jaxpr/ppermute | solution.py:23
  72.9 10.9 %collective-permute-start.1 = (bf16[512,512]{1,0:T(8,128)(2,1)S(1)}, bf16[512,512]{1,0:T(8,128)(2,1)S(1)}, u32[]{:S(2)}, u32[]{:S(2)}) collective-permute-start(bf16[512,512]{1,0:T(8,128)(2,1)S(1)} %dynamic-slice_select_fusion.2), channel_id=1, source_target_pairs={{0,1},{1,2},{2,3},{3,4},{4,5},{5,6},{6,7},{7,0},{8,9},{9,10},{10,1... | collective-permute-start | bytes 1572872 | tf_op jit(solution)/shard_map/while/body/eval_jaxpr/ppermute | solution.py:14
  74.6 13.2 %collective-permute-start.2 = (bf16[512,512]{1,0:T(8,128)(2,1)S(1)}, bf16[512,512]{1,0:T(8,128)(2,1)S(1)}, u32[]{:S(2)}, u32[]{:S(2)}) collective-permute-start(bf16[512,512]{1,0:T(8,128)(2,1)S(1)} %dynamic-slice_select_fusion.2), channel_id=1, source_target_pairs={{1,0},{2,1},{3,2},{4,3},{5,4},{6,5},{7,6},{0,7},{9,8},{10,9},{11,1... | collective-permute-start | bytes 1572872 | tf_op jit(solution)/shard_map/while/body/eval_jaxpr/ppermute | solution.py:15
  101.1 13.7 %collective-permute-start = (bf16[512,512]{1,0:T(8,128)(2,1)S(1)}, bf16[512,512]{1,0:T(8,128)(2,1)S(1)}, u32[]{:S(2)}, u32[]{:S(2)}) collective-permute-start(bf16[512,512]{1,0:T(8,128)(2,1)S(1)} %broadcast_select_fusion.2), channel_id=1, source_target_pairs={{0,8},{8,16},{16,24},{1,9},{9,17},{17,25},{2,10},{10,18},{18,26},{... | collective-permute-start | bytes 1572872 | tf_op jit(solution)/shard_map/while/body/eval_jaxpr/ppermute | solution.py:23
  116.0 14.6 %collective-permute-start.1 = (bf16[512,512]{1,0:T(8,128)(2,1)S(1)}, bf16[512,512]{1,0:T(8,128)(2,1)S(1)}, u32[]{:S(2)}, u32[]{:S(2)}) collective-permute-start(bf16[512,512]{1,0:T(8,128)(2,1)S(1)} %dynamic-slice_select_fusion.2), channel_id=1, source_target_pairs={{0,1},{1,2},{2,3},{3,4},{4,5},{5,6},{6,7},{7,0},{8,9},{9,10},{10,1... | collective-permute-start | bytes 1572872 | tf_op jit(solution)/shard_map/while/body/eval_jaxpr/ppermute | solution.py:14
  120.8 13.6 %collective-permute-start.2 = (bf16[512,512]{1,0:T(8,128)(2,1)S(1)}, bf16[512,512]{1,0:T(8,128)(2,1)S(1)}, u32[]{:S(2)}, u32[]{:S(2)}) collective-permute-start(bf16[512,512]{1,0:T(8,128)(2,1)S(1)} %dynamic-slice_select_fusion.2), channel_id=1, source_target_pairs={{1,0},{2,1},{3,2},{4,3},{5,4},{6,5},{7,6},{0,7},{9,8},{10,9},{11,1... | collective-permute-start | bytes 1572872 | tf_op jit(solution)/shard_map/while/body/eval_jaxpr/ppermute | solution.py:15
  147.7 14.6 %collective-permute-start = (bf16[512,512]{1,0:T(8,128)(2,1)S(1)}, bf16[512,512]{1,0:T(8,128)(2,1)S(1)}, u32[]{:S(2)}, u32[]{:S(2)}) collective-permute-start(bf16[512,512]{1,0:T(8,128)(2,1)S(1)} %broadcast_select_fusion.2), channel_id=1, source_target_pairs={{0,8},{8,16},{16,24},{1,9},{9,17},{17,25},{2,10},{10,18},{18,26},{... | collective-permute-start | bytes 1572872 | tf_op jit(solution)/shard_map/while/body/eval_jaxpr/ppermute | solution.py:23
  164.4 11.4 %collective-permute-start.2 = (bf16[512,512]{1,0:T(8,128)(2,1)S(1)}, bf16[512,512]{1,0:T(8,128)(2,1)S(1)}, u32[]{:S(2)}, u32[]{:S(2)}) collective-permute-start(bf16[512,512]{1,0:T(8,128)(2,1)S(1)} %dynamic-slice_select_fusion.2), channel_id=1, source_target_pairs={{1,0},{2,1},{3,2},{4,3},{5,4},{6,5},{7,6},{0,7},{9,8},{10,9},{11,1... | collective-permute-start | bytes 1572872 | tf_op jit(solution)/shard_map/while/body/eval_jaxpr/ppermute | solution.py:15
  189.1 9.9 %collective-permute-start = (bf16[512,512]{1,0:T(8,128)(2,1)S(1)}, bf16[512,512]{1,0:T(8,128)(2,1)S(1)}, u32[]{:S(2)}, u32[]{:S(2)}) collective-permute-start(bf16[512,512]{1,0:T(8,128)(2,1)S(1)} %broadcast_select_fusion.2), channel_id=1, source_target_pairs={{0,8},{8,16},{16,24},{1,9},{9,17},{17,25},{2,10},{10,18},{18,26},{... | collective-permute-start | bytes 1572872 | tf_op jit(solution)/shard_map/while/body/eval_jaxpr/ppermute | solution.py:23
  200.2 19.0 %collective-permute-start.1 = (bf16[512,512]{1,0:T(8,128)(2,1)S(1)}, bf16[512,512]{1,0:T(8,128)(2,1)S(1)}, u32[]{:S(2)}, u32[]{:S(2)}) collective-permute-start(bf16[512,512]{1,0:T(8,128)(2,1)S(1)} %dynamic-slice_select_fusion.2), channel_id=1, source_target_pairs={{0,1},{1,2},{2,3},{3,4},{4,5},{5,6},{6,7},{7,0},{8,9},{9,10},{10,1... | collective-permute-start | bytes 1572872 | tf_op jit(solution)/shard_map/while/body/eval_jaxpr/ppermute | solution.py:14
  209.4 13.7 %collective-permute-start.2 = (bf16[512,512]{1,0:T(8,128)(2,1)S(1)}, bf16[512,512]{1,0:T(8,128)(2,1)S(1)}, u32[]{:S(2)}, u32[]{:S(2)}) collective-permute-start(bf16[512,512]{1,0:T(8,128)(2,1)S(1)} %dynamic-slice_select_fusion.2), channel_id=1, source_target_pairs={{1,0},{2,1},{3,2},{4,3},{5,4},{6,5},{7,6},{0,7},{9,8},{10,9},{11,1... | collective-permute-start | bytes 1572872 | tf_op jit(solution)/shard_map/while/body/eval_jaxpr/ppermute | solution.py:15
  236.4 13.6 %collective-permute-start = (bf16[512,512]{1,0:T(8,128)(2,1)S(1)}, bf16[512,512]{1,0:T(8,128)(2,1)S(1)}, u32[]{:S(2)}, u32[]{:S(2)}) collective-permute-start(bf16[512,512]{1,0:T(8,128)(2,1)S(1)} %broadcast_select_fusion.2), channel_id=1, source_target_pairs={{0,8},{8,16},{16,24},{1,9},{9,17},{17,25},{2,10},{10,18},{18,26},{... | collective-permute-start | bytes 1572872 | tf_op jit(solution)/shard_map/while/body/eval_jaxpr/ppermute | solution.py:23
  251.2 12.0 %collective-permute-start.1 = (bf16[512,512]{1,0:T(8,128)(2,1)S(1)}, bf16[512,512]{1,0:T(8,128)(2,1)S(1)}, u32[]{:S(2)}, u32[]{:S(2)}) collective-permute-start(bf16[512,512]{1,0:T(8,128)(2,1)S(1)} %dynamic-slice_select_fusion.2), channel_id=1, source_target_pairs={{0,1},{1,2},{2,3},{3,4},{4,5},{5,6},{6,7},{7,0},{8,9},{9,10},{10,1... | collective-permute-start | bytes 1572872 | tf_op jit(solution)/shard_map/while/body/eval_jaxpr/ppermute | solution.py:14
  252.9 14.2 %collective-permute-start.2 = (bf16[512,512]{1,0:T(8,128)(2,1)S(1)}, bf16[512,512]{1,0:T(8,128)(2,1)S(1)}, u32[]{:S(2)}, u32[]{:S(2)}) collective-permute-start(bf16[512,512]{1,0:T(8,128)(2,1)S(1)} %dynamic-slice_select_fusion.2), channel_id=1, source_target_pairs={{1,0},{2,1},{3,2},{4,3},{5,4},{6,5},{7,6},{0,7},{9,8},{10,9},{11,1... | collective-permute-start | bytes 1572872 | tf_op jit(solution)/shard_map/while/body/eval_jaxpr/ppermute | solution.py:15
  280.3 13.1 %collective-permute-start = (bf16[512,512]{1,0:T(8,128)(2,1)S(1)}, bf16[512,512]{1,0:T(8,128)(2,1)S(1)}, u32[]{:S(2)}, u32[]{:S(2)}) collective-permute-start(bf16[512,512]{1,0:T(8,128)(2,1)S(1)} %broadcast_select_fusion.2), channel_id=1, source_target_pairs={{0,8},{8,16},{16,24},{1,9},{9,17},{17,25},{2,10},{10,18},{18,26},{... | collective-permute-start | bytes 1572872 | tf_op jit(solution)/shard_map/while/body/eval_jaxpr/ppermute | solution.py:23
  294.6 13.0 %collective-permute-start.1 = (bf16[512,512]{1,0:T(8,128)(2,1)S(1)}, bf16[512,512]{1,0:T(8,128)(2,1)S(1)}, u32[]{:S(2)}, u32[]{:S(2)}) collective-permute-start(bf16[512,512]{1,0:T(8,128)(2,1)S(1)} %dynamic-slice_select_fusion.2), channel_id=1, source_target_pairs={{0,1},{1,2},{2,3},{3,4},{4,5},{5,6},{6,7},{7,0},{8,9},{9,10},{10,1... | collective-permute-start | bytes 1572872 | tf_op jit(solution)/shard_map/while/body/eval_jaxpr/ppermute | solution.py:14
  296.8 14.7 %collective-permute-start.2 = (bf16[512,512]{1,0:T(8,128)(2,1)S(1)}, bf16[512,512]{1,0:T(8,128)(2,1)S(1)}, u32[]{:S(2)}, u32[]{:S(2)}) collective-permute-start(bf16[512,512]{1,0:T(8,128)(2,1)S(1)} %dynamic-slice_select_fusion.2), channel_id=1, source_target_pairs={{1,0},{2,1},{3,2},{4,3},{5,4},{6,5},{7,6},{0,7},{9,8},{10,9},{11,1... | collective-permute-start | bytes 1572872 | tf_op jit(solution)/shard_map/while/body/eval_jaxpr/ppermute | solution.py:15
  324.8 12.6 %collective-permute-start = (bf16[512,512]{1,0:T(8,128)(2,1)S(1)}, bf16[512,512]{1,0:T(8,128)(2,1)S(1)}, u32[]{:S(2)}, u32[]{:S(2)}) collective-permute-start(bf16[512,512]{1,0:T(8,128)(2,1)S(1)} %broadcast_select_fusion.2), channel_id=1, source_target_pairs={{0,8},{8,16},{16,24},{1,9},{9,17},{17,25},{2,10},{10,18},{18,26},{... | collective-permute-start | bytes 1572872 | tf_op jit(solution)/shard_map/while/body/eval_jaxpr/ppermute | solution.py:23
  338.6 13.3 %collective-permute-start.1 = (bf16[512,512]{1,0:T(8,128)(2,1)S(1)}, bf16[512,512]{1,0:T(8,128)(2,1)S(1)}, u32[]{:S(2)}, u32[]{:S(2)}) collective-permute-start(bf16[512,512]{1,0:T(8,128)(2,1)S(1)} %dynamic-slice_select_fusion.2), channel_id=1, source_target_pairs={{0,1},{1,2},{2,3},{3,4},{4,5},{5,6},{6,7},{7,0},{8,9},{9,10},{10,1... | collective-permute-start | bytes 1572872 | tf_op jit(solution)/shard_map/while/body/eval_jaxpr/ppermute | solution.py:14
  341.3 14.6 %collective-permute-start.2 = (bf16[512,512]{1,0:T(8,128)(2,1)S(1)}, bf16[512,512]{1,0:T(8,128)(2,1)S(1)}, u32[]{:S(2)}, u32[]{:S(2)}) collective-permute-start(bf16[512,512]{1,0:T(8,128)(2,1)S(1)} %dynamic-slice_select_fusion.2), channel_id=1, source_target_pairs={{1,0},{2,1},{3,2},{4,3},{5,4},{6,5},{7,6},{0,7},{9,8},{10,9},{11,1... | collective-permute-start | bytes 1572872 | tf_op jit(solution)/shard_map/while/body/eval_jaxpr/ppermute | solution.py:15
  (2 other events, 14.5 us)
where the time goes:
time: 374 us; the launch traced here: 369 us
  waiting for transfers between devices  176 us (47%)
  other arithmetic  56.4 us (15%)
  local copies, waits for them, and re-layouts  46.8 us (13%)
  matrix products  39.1 us (10%)
  starting transfers between devices  31.6 us (8%)
  loops' own time  19.2 us (5%)
    ppermute x9, waiting for transfers between devices, with_halo(): before = lax.ppermute(last, axis, up)  98.8 us
    ppermute x7, waiting for transfers between devices, passed_along(): return lax.ppermute(x, axis, pairs)  73.7 us
    dynamic_update_slice x21, other arithmetic, place(): lax.dynamic_update_slice_in_dim(target, jnp.where(active, piece, previous...  41.6 us
    gather x7, local copies, waits for them, and re-layouts, compute(): sources = buffer.reshape(3 * blocks_part, block_side, width)[index_group]  39.3 us
    dot_general x7, matrix products, compute(): jnp.einsum('rkij,rkjd->rid', tile_group, sources, preferred_element_type=...  22.6 us
    ppermute x9, starting transfers between devices, with_halo(): before = lax.ppermute(last, axis, up)  19.7 us
    another operation x1, loops' own time, on_device(): lax.fori_loop(0, step_count, advance, (outgoing_start, buffer_start, hidd...  19.2 us
    dot_general x7, matrix products, compute(): product = jnp.dot(aggregate, weight, preferred_element_type=jnp.float32)  16.5 us
  transfers between devices with their start and end apart: 25, of which 18 were waited for; matrix products, arithmetic and copies ran while one was open for 9% of the time, Pallas kernels for 0%

commit v1 on v0

v1 whole, which is shorter than its diff:
```python
import functools

import jax
import jax.numpy as jnp
from jax import lax
from jax.experimental import pallas as pl
from jax.experimental.pallas import tpu as pltpu
from jax.sharding import PartitionSpec as P

MESH = pl.DeviceIdType.MESH


def pipeline_kernel(
    sections, parts, groups, table, order, x_ref, adj_hbm, w_ref, out_ref,
    adj, src, mine, own_land, side_land,
    adj_sem, stale_send, stale_recv, z_send, z_recv, f_send, f_recv,
):
    s = lax.axis_index("section")
    d = lax.axis_index("dom")
    right, left = lax.rem(d + 1, parts), lax.rem(d + parts - 1, parts)
    blocks, side, width = x_ref.shape
    tiles = adj.shape[1]
    bg = blocks // groups
    fresh = 3 * blocks
    last = sections - 1

    load_adj = pltpu.make_async_copy(adj_hbm, adj, adj_sem)
    load_adj.start()

    for k in range(groups):
        piece = x_ref[pl.ds(order[k] * bg, bg)]
        mine[k * bg:(k + 1) * bg] = piece
        src[blocks + k * bg:blocks + (k + 1) * bg] = piece

    barrier = pltpu.get_barrier_semaphore()
    for neighbour in (left, right):
        pl.semaphore_signal(barrier, inc=1, device_id={"dom": neighbour}, device_id_type=MESH)

    @pl.when(s > 0)
    def _():
        pl.semaphore_signal(barrier, inc=1, device_id={"section": s - 1}, device_id_type=MESH)

    @pl.when(s < last)
    def _():
        pl.semaphore_signal(barrier, inc=1, device_id={"section": s + 1}, device_id_type=MESH)

    peers = 2 + jnp.where(s > 0, 1, 0) + jnp.where(s < last, 1, 0)
    pl.semaphore_wait(barrier, peers)

    def stale_copy(way, k):
        base = (0 if way == 0 else 2 * blocks) + k * bg
        return pltpu.make_async_remote_copy(
            src_ref=mine.at[pl.ds(k * bg, bg)],
            dst_ref=src.at[pl.ds(base, bg)],
            send_sem=stale_send.at[way, k],
            recv_sem=stale_recv.at[way, k],
            device_id={"dom": right if way == 0 else left},
            device_id_type=MESH,
        )

    def side_copy(way, r):
        return pltpu.make_async_remote_copy(
            src_ref=own_land.at[r],
            dst_ref=side_land.at[way, r],
            send_sem=f_send.at[way, r],
            recv_sem=f_recv.at[way, r],
            device_id={"dom": right if way == 0 else left},
            device_id_type=MESH,
        )

    def up_copy(r):
        return pltpu.make_async_remote_copy(
            src_ref=out_ref.at[r],
            dst_ref=own_land.at[r],
            send_sem=z_send.at[r],
            recv_sem=z_recv.at[r],
            device_id={"section": jnp.minimum(s + 1, last)},
            device_id_type=MESH,
        )

    @pl.when(s == 0)
    def _():
        for way in range(2):
            stale_copy(way, 0).start()

    for k in range(1, groups):
        for way in range(2):
            stale_copy(way, k).start()

    load_adj.wait()
    own_base = jnp.where(s > 0, fresh + blocks, blocks)

    for k in range(groups):
        lo, hi = k * bg, (k + 1) * bg

        @pl.when(s > 0)
        def _():
            @pl.loop(lo, hi)
            def _(r):
                up_copy(r).wait_recv()
                side_copy(0, r).start()
                side_copy(1, r).start()

            src[fresh + blocks + lo:fresh + blocks + hi] = own_land[lo:hi]

            @pl.loop(lo, hi)
            def _(r):
                side_copy(0, r).wait_recv()
                side_copy(1, r).wait_recv()

            src[fresh + lo:fresh + hi] = side_land[0, lo:hi]
            src[fresh + 2 * blocks + lo:fresh + 2 * blocks + hi] = side_land[1, lo:hi]

        if k == 0:
            @pl.when(s == 0)
            def _():
                for way in range(2):
                    stale_copy(way, 0).wait_recv()

            for q in range(1, groups):
                for way in range(2):
                    stale_copy(way, q).wait_recv()

        @pl.loop(lo, hi)
        def _(r):
            row = order[k] * bg + (r - lo)
            a = jnp.concatenate([adj[row, t] for t in range(tiles)], axis=1)
            h = jnp.concatenate([src[table[r * tiles + t]] for t in range(tiles)], axis=0)
            agg = jnp.dot(a, h, preferred_element_type=jnp.float32).astype(jnp.bfloat16)
            product = jnp.dot(agg, w_ref[...], preferred_element_type=jnp.float32)
            before = src[own_base + r].astype(jnp.float32)
            out_ref[r] = (before + jnp.maximum(product, 0.0)).astype(jnp.bfloat16)

            @pl.when(s < last)
            def _():
                up_copy(r).start()

    for k in range(1, groups):
        for way in range(2):
            stale_copy(way, k).wait_send()

    @pl.when(s == 0)
    def _():
        for way in range(2):
            stale_copy(way, 0).wait_send()

    @pl.when(s > 0)
    def _():
        @pl.loop(0, blocks)
        def _(r):
            side_copy(0, r).wait_send()
            side_copy(1, r).wait_send()

    @pl.when(s < last)
    def _():
        @pl.loop(0, blocks)
        def _(r):
            up_copy(r).wait_send()


def place_kernel(where, h_ref, out_ref):
    out_ref[...] = h_ref[...]


def on_device(sections, layer_inputs, adjacency, columns, group_order, weights):
    parts = lax.axis_size("dom")
    d = lax.axis_index("dom")
    s = lax.axis_index("section")
    rows, width = layer_inputs.shape[1:]
    blocks, tiles, side = adjacency.shape[:3]
    groups = group_order.shape[1]
    bg = blocks // groups
    up = [(i, (i + 1) % parts) for i in range(parts)]
    down = [(j, i) for i, j in up]
    before = lax.ppermute(group_order, "dom", up)
    after = lax.ppermute(group_order, "dom", down)
    orders = jnp.concatenate([before, group_order, after], axis=0)
    ids = jnp.arange(groups, dtype=jnp.int32)
    position = jnp.sum(
        jnp.where(orders[:, :, None] == ids[None, None, :], ids[None, :, None], 0), axis=1
    ).astype(jnp.int32)
    relative = (columns // blocks - d + 1) % parts
    inside = columns % blocks
    key = relative * groups + inside // bg
    flat = position.reshape(-1)
    hits = key[:, :, None] == jnp.arange(3 * groups, dtype=jnp.int32)[None, None, :]
    tile_pos = jnp.sum(jnp.where(hits, flat[None, None, :], 0), axis=2)
    row_pos = jnp.repeat(position[1], bg)
    is_fresh = (tile_pos <= row_pos[:, None]) & (s > 0)
    slot = relative * blocks + tile_pos * bg + inside % bg + jnp.where(is_fresh, 3 * blocks, 0)
    by_pos = slot.reshape(groups, bg, tiles)
    pick = group_order[0][:, None] == ids[None, :]
    table = jnp.sum(jnp.where(pick[:, :, None, None], by_pos[None], 0), axis=1)
    table = table.reshape(-1).astype(jnp.int32)

    dma = pltpu.SemaphoreType.DMA
    hidden = pl.pallas_call(
        functools.partial(pipeline_kernel, sections, parts, groups),
        out_shape=jax.ShapeDtypeStruct((blocks, side, width), jnp.bfloat16),
        in_specs=[
            pl.BlockSpec(memory_space=pltpu.SMEM),
            pl.BlockSpec(memory_space=pltpu.SMEM),
            pl.BlockSpec(memory_space=pltpu.VMEM),
            pl.BlockSpec(memory_space=pl.ANY),
            pl.BlockSpec(memory_space=pltpu.VMEM),
        ],
        out_specs=pl.BlockSpec(memory_space=pltpu.VMEM),
        scratch_shapes=[
            pltpu.VMEM(adjacency.shape, jnp.bfloat16),
            pltpu.VMEM((6 * blocks, side, width), jnp.bfloat16),
            pltpu.VMEM((blocks, side, width), jnp.bfloat16),
            pltpu.VMEM((blocks, side, width), jnp.bfloat16),
            pltpu.VMEM((2, blocks, side, width), jnp.bfloat16),
            dma,
            dma((2, groups)),
            dma((2, groups)),
            dma((blocks,)),
            dma((blocks,)),
            dma((2, blocks)),
            dma((2, blocks)),
        ],
        compiler_params=pltpu.CompilerParams(
            collective_id=0, has_side_effects=True, vmem_limit_bytes=56 * 2**20
        ),
    )(table, group_order[0], layer_inputs.reshape(blocks, side, width), adjacency, weights[0])

    placed = pl.pallas_call(
        place_kernel,
        out_shape=jax.ShapeDtypeStruct((blocks, side, width), jnp.bfloat16),
        grid_spec=pltpu.PrefetchScalarGridSpec(
            num_scalar_prefetch=1,
            grid=(groups,),
            in_specs=[pl.BlockSpec((bg, side, width), lambda k, o: (k, 0, 0))],
            out_specs=pl.BlockSpec((bg, side, width), lambda k, o: (o[k], 0, 0)),
        ),
    )(group_order[0], hidden)
    return placed.reshape(1, rows, width)


def solution(mesh):
    in_specs = (
        P("section", "dom", None),
        P("dom", None, None, None),
        P("dom", None),
        P("dom", None),
        P("section", None, None),
    )
    return jax.shard_map(
        functools.partial(on_device, mesh.shape["section"]),
        mesh=mesh, in_specs=in_specs, out_specs=P("section", "dom", None), check_vma=False,
    )
```

time: 374 us -> 160 us (0.43); the launches traced: 369 us -> 159 us
  waiting for transfers between devices: 176 us -> 2.55 us
  Pallas kernels: 0 us -> 151 us
  other arithmetic: 56.4 us -> 3.11 us
  local copies, waits for them, and re-layouts: 46.8 us -> 0.93 us
  matrix products: 39.1 us -> 0 us
  starting transfers between devices: 31.6 us -> 1.77 us
  loops' own time: 19.2 us -> 0 us
    ppermute x25 -> x2, waiting for transfers between devices: 176 us -> 2.55 us  [the longest x1 2.55 us: on_device(): after = lax.ppermute(group_order, 'dom', down)]
    pallas_call x0 -> x2, Pallas kernels: none -> 151 us  [the longest x1 147 us: on_device(): pl.pallas_call(functools.partial(pipeline_kernel, sections, parts, groups...]
    dynamic_update_slice x21 -> x0, other arithmetic: 41.6 us -> none  [place(): lax.dynamic_update_slice_in_dim(target, jnp.where(active, piece, previous...]
    gather x7 -> x0, local copies, waits for them, and re-layouts: 39.3 us -> none  [compute(): sources = buffer.reshape(3 * blocks_part, block_side, width)[index_group]]
    dot_general x14 -> x0, matrix products: 39.1 us -> none  [the longest x7 22.6 us: compute(): jnp.einsum('rkij,rkjd->rid', tile_group, sources, preferred_element_type=...]
    ppermute x25 -> x2, starting transfers between devices: 31.6 us -> 1.77 us  [the longest x1 1.77 us: on_device(): before = lax.ppermute(group_order, 'dom', up)]
    another operation x1 -> x0, loops' own time: 19.2 us -> none  [on_device(): lax.fori_loop(0, step_count, advance, (outgoing_start, buffer_start, hidd...]
    select_n x14 -> x0, other arithmetic: 8.31 us -> none  [the longest x7 8.23 us: advance(): group_in = jnp.where(my_section == 0, own_stored, arrived)]
  transfers between devices with their start and end apart: 25 -> 2, of which waited for: 18 -> 1; matrix products, arithmetic and copies ran while one was open for 9% -> 1% of each run, Pallas kernels for 0% -> 0%
where the time goes in v1:
time: 160 us; the launch traced here: 159 us
  Pallas kernels  151 us (94%)
  other arithmetic  3.11 us (2%)
  waiting for transfers between devices  2.55 us (2%)
  starting transfers between devices  1.77 us (1%)
    pallas_call x1, Pallas kernels, on_device(): pl.pallas_call(functools.partial(pipeline_kernel, sections, parts, groups...  147 us
    pallas_call x1, Pallas kernels, on_device(): pl.pallas_call(place_kernel, out_shape=jax.ShapeDtypeStruct((blocks, side...  4.45 us
  transfers between devices with their start and end apart: 2, of which 1 were waited for; matrix products, arithmetic and copies ran while one was open for 1% of the time, Pallas kernels for 0%

profile of v1, /device:TPU:27, one launch (start us, length us, event | category | flops | bytes accessed | tf_op | source)
XLA Modules:
  0.0 159.4 jit_solution(10845803727800447226)
XLA Ops:
  0.0 1.8 %collective-permute-start = (s32[1,4]{1,0:T(1,128)}, s32[1,4]{1,0:T(1,128)S(1)}, u32[]{:S(2)}, u32[]{:S(2)}) collective-permute-start(s32[1,4]{1,0:T(1,128)} %param.8), channel_id=1, source_target_pairs={{0,1},{1,2},{2,3},{3,4},{4,5},{5,6},{6,7},{7,0},{8,9},{9,10},{10,1... | collective-permute-start | bytes 56 | tf_op jit(solution)/shard_map/ppermute | solution.py:175
  1.8 0.0 collective-permute-start.1
  1.8 0.8 iota_compare_fusion.2
  2.5 0.7 fusion.3
  3.2 0.0 collective-permute-done
  3.3 2.5 %collective-permute-done.1 = s32[1,4]{1,0:T(1,128)S(1)} collective-permute-done((s32[1,4]{1,0:T(1,128)}, s32[1,4]{1,0:T(1,128)S(1)}, u32[]{:S(2)}, u32[]{:S(2)}) %collective-permute-start.1) | collective-permute-done | bytes 48 | tf_op jit(solution)/shard_map/ppermute | solution.py:176
  5.8 0.7 pad_add_fusion
  6.5 0.1 select_reduce_fusion.2
  6.6 0.1 broadcast_in_dim.67
  6.6 0.1 broadcast_in_dim.70
  6.7 0.1 le.10
  6.8 0.1 select_reduce_fusion
  6.9 0.7 fusion.5
  7.6 0.1 copy.10
  7.7 0.1 select_reduce_fusion.1
  7.8 0.6 reshape.38.table
  8.4 146.6 %shard_map.55.h_ref = bf16[16,128,512]{2,1,0:T(8,128)(2,1)} custom-call(s32[128]{0:T(128)} %reshape.38.table, s32[4]{0:T(128)} %bitcast.11, bf16[16,128,512]{2,1,0:T(8,128)(2,1)} %bitcast.7, bf16[16,8,128,128]{3,2,1,0:T(8,128)(2,1)} %adj_hbm.1, bf16[512,512]{1,0:T(8,128)(2,1)} %bitcast.8), custom_call_target="tpu_custom_call" | custom-call | tf_op jit(solution)/shard_map/pallas_call | solution.py:197
  155.0 4.5 %shard_map.56 = bf16[16,128,512]{2,1,0:T(8,128)(2,1)} custom-call(s32[4]{0:T(128)} %bitcast.12, bf16[16,128,512]{2,1,0:T(8,128)(2,1)} %shard_map.55.h_ref), custom_call_target="tpu_custom_call" | custom-call | tf_op jit(solution)/shard_map/pallas_call | solution.py:227
  (1 shorter events, 0.0 us)
Async XLA Ops:
  0.0 3.2 %collective-permute-start = (s32[1,4]{1,0:T(1,128)}, s32[1,4]{1,0:T(1,128)S(1)}, u32[]{:S(2)}, u32[]{:S(2)}) collective-permute-start(s32[1,4]{1,0:T(1,128)} %param.8), channel_id=1, source_target_pairs={{0,1},{1,2},{2,3},{3,4},{4,5},{5,6},{6,7},{7,0},{8,9},{9,10},{10,1... | collective-permute-start | bytes 56 | tf_op jit(solution)/shard_map/ppermute | solution.py:175
  1.8 4.0 %collective-permute-start.1 = (s32[1,4]{1,0:T(1,128)}, s32[1,4]{1,0:T(1,128)S(1)}, u32[]{:S(2)}, u32[]{:S(2)}) collective-permute-start(s32[1,4]{1,0:T(1,128)} %param.8), channel_id=1, source_target_pairs={{1,0},{2,1},{3,2},{4,3},{5,4},{6,5},{7,6},{0,7},{9,8},{10,9},{11,1... | collective-permute-start | bytes 56 | tf_op jit(solution)/shard_map/ppermute | solution.py:176

commit v2 on v1

--- a/solution.py
+++ b/solution.py
@@ -10,10 +10,16 @@
 MESH = pl.DeviceIdType.MESH
 
 
+def relay_plan(sections, blocks):
+    far, near = blocks // 4, blocks // 8
+    return ((sections - 1, 0, far), (sections - 2, far, near))
+
+
 def pipeline_kernel(
     sections, parts, groups, table, order, x_ref, adj_hbm, w_ref, out_ref,
-    adj, src, mine, own_land, side_land,
+    adj, src, mine, own_land, side_land, relay_up, relay_over,
     adj_sem, stale_send, stale_recv, z_send, z_recv, f_send, f_recv,
+    up_send, up_recv, over_send, over_recv, down_send, down_recv,
 ):
     s = lax.axis_index("section")
     d = lax.axis_index("dom")
@@ -23,6 +29,12 @@
     bg = blocks // groups
     fresh = 3 * blocks
     last = sections - 1
+    odd = lax.rem(d, 2)
+    across = lax.rem(d + parts - 1 + 2 * odd, parts)
+    from_across = jnp.where(odd == 1, 2 * blocks, 0)
+    relays = relay_plan(sections, blocks)
+    relayed = sum(count for _, _, count in relays)
+    direct = blocks - relayed
 
     load_adj = pltpu.make_async_copy(adj_hbm, adj, adj_sem)
     load_adj.start()
@@ -45,6 +57,17 @@
         pl.semaphore_signal(barrier, inc=1, device_id={"section": s + 1}, device_id_type=MESH)
 
     peers = 2 + jnp.where(s > 0, 1, 0) + jnp.where(s < last, 1, 0)
+    for plane, _, _ in relays:
+        peers = peers + jnp.where(s == 0, 1, 0) + jnp.where(s == plane, 1, 0)
+
+        @pl.when(s == 0)
+        def _():
+            pl.semaphore_signal(barrier, inc=1, device_id={"section": plane}, device_id_type=MESH)
+
+        @pl.when(s == plane)
+        def _():
+            pl.semaphore_signal(barrier, inc=1, device_id={"section": 0}, device_id_type=MESH)
+
     pl.semaphore_wait(barrier, peers)
 
     def stale_copy(way, k):
@@ -78,14 +101,92 @@
             device_id_type=MESH,
         )
 
+    def partner_copy():
+        return pltpu.make_async_remote_copy(
+            src_ref=mine,
+            dst_ref=src.at[pl.ds(jnp.where(odd == 1, 2 * blocks, 0), blocks)],
+            send_sem=stale_send.at[0, 0],
+            recv_sem=stale_recv.at[0, 0],
+            device_id={"dom": jnp.where(odd == 1, left, right)},
+            device_id_type=MESH,
+        )
+
+    def across_copy():
+        return pltpu.make_async_remote_copy(
+            src_ref=mine.at[pl.ds(0, direct)],
+            dst_ref=src.at[pl.ds(jnp.where(odd == 1, 0, 2 * blocks), direct)],
+            send_sem=stale_send.at[1, 0],
+            recv_sem=stale_recv.at[1, 0],
+            device_id={"dom": across},
+            device_id_type=MESH,
+        )
+
+    def relay_up_copy(plane, b):
+        return pltpu.make_async_remote_copy(
+            src_ref=mine.at[direct + b],
+            dst_ref=relay_up.at[b],
+            send_sem=up_send.at[b],
+            recv_sem=up_recv.at[b],
+            device_id={"section": plane},
+            device_id_type=MESH,
+        )
+
+    def relay_over_copy(b):
+        return pltpu.make_async_remote_copy(
+            src_ref=relay_up.at[b],
+            dst_ref=relay_over.at[b],
+            send_sem=over_send.at[b],
+            recv_sem=over_recv.at[b],
+            device_id={"dom": across},
+            device_id_type=MESH,
+        )
+
+    def relay_down_copy(b):
+        return pltpu.make_async_remote_copy(
+            src_ref=relay_over.at[b],
+            dst_ref=src.at[from_across + direct + b],
+            send_sem=down_send.at[b],
+            recv_sem=down_recv.at[b],
+            device_id={"section": 0},
+            device_id_type=MESH,
+        )
+
     @pl.when(s == 0)
     def _():
-        for way in range(2):
-            stale_copy(way, 0).start()
-
-    for k in range(1, groups):
-        for way in range(2):
-            stale_copy(way, k).start()
+        across_copy().start()
+        for plane, first, count in relays:
+            @pl.loop(first, first + count)
+            def _(b):
+                relay_up_copy(plane, b).start()
+
+        partner_copy().start()
+
+    for plane, first, count in relays:
+        @pl.when(s == plane)
+        def _():
+            @pl.loop(first, first + count)
+            def _(b):
+                relay_up_copy(plane, b).wait_recv()
+                relay_over_copy(b).start()
+
+            for k in range(1, groups):
+                for way in range(2):
+                    stale_copy(way, k).start()
+
+            @pl.loop(first, first + count)
+            def _(b):
+                relay_over_copy(b).wait_recv()
+                relay_down_copy(b).start()
+
+    plain = s > 0
+    for plane, _, _ in relays:
+        plain = plain & (s != plane)
+
+    @pl.when(plain)
+    def _():
+        for k in range(1, groups):
+            for way in range(2):
+                stale_copy(way, k).start()
 
     load_adj.wait()
     own_base = jnp.where(s > 0, fresh + blocks, blocks)
@@ -114,12 +215,18 @@
         if k == 0:
             @pl.when(s == 0)
             def _():
-                for way in range(2):
-                    stale_copy(way, 0).wait_recv()
-
-            for q in range(1, groups):
-                for way in range(2):
-                    stale_copy(way, q).wait_recv()
+                partner_copy().wait_recv()
+                across_copy().wait_recv()
+
+                @pl.loop(0, relayed)
+                def _(b):
+                    relay_down_copy(b).wait_recv()
+
+            @pl.when(s > 0)
+            def _():
+                for q in range(1, groups):
+                    for way in range(2):
+                        stale_copy(way, q).wait_recv()
 
         @pl.loop(lo, hi)
         def _(r):
@@ -135,17 +242,29 @@
             def _():
                 up_copy(r).start()
 
-    for k in range(1, groups):
-        for way in range(2):
-            stale_copy(way, k).wait_send()
-
     @pl.when(s == 0)
     def _():
-        for way in range(2):
-            stale_copy(way, 0).wait_send()
+        partner_copy().wait_send()
+        across_copy().wait_send()
+        for plane, first, count in relays:
+            @pl.loop(first, first + count)
+            def _(b):
+                relay_up_copy(plane, b).wait_send()
+
+    for plane, first, count in relays:
+        @pl.when(s == plane)
+        def _():
+            @pl.loop(first, first + count)
+            def _(b):
+                relay_over_copy(b).wait_send()
+                relay_down_copy(b).wait_send()
 
     @pl.when(s > 0)
     def _():
+        for k in range(1, groups):
+            for way in range(2):
+                stale_copy(way, k).wait_send()
+
         @pl.loop(0, blocks)
         def _(r):
             side_copy(0, r).wait_send()
@@ -158,8 +277,25 @@
             up_copy(r).wait_send()
 
 
-def place_kernel(where, h_ref, out_ref):
-    out_ref[...] = h_ref[...]
+def place_kernel(groups, order, h_hbm, out_hbm, held, in_sem, out_sem):
+    bg = h_hbm.shape[0] // groups
+
+    def load(k):
+        rows = pl.ds(k * bg, bg)
+        return pltpu.make_async_copy(h_hbm.at[rows], held.at[rows], in_sem.at[k])
+
+    def store(k):
+        return pltpu.make_async_copy(
+            held.at[pl.ds(k * bg, bg)], out_hbm.at[pl.ds(order[k] * bg, bg)], out_sem.at[k]
+        )
+
+    for k in range(groups):
+        load(k).start()
+    for k in range(groups):
+        load(k).wait()
+        store(k).start()
+    for k in range(groups):
+        store(k).wait()
 
 
 def on_device(sections, layer_inputs, adjacency, columns, group_order, weights):
@@ -193,6 +329,7 @@
     table = jnp.sum(jnp.where(pick[:, :, None, None], by_pos[None], 0), axis=1)
     table = table.reshape(-1).astype(jnp.int32)
 
+    relayed = sum(count for _, _, count in relay_plan(sections, blocks))
     dma = pltpu.SemaphoreType.DMA
     hidden = pl.pallas_call(
         functools.partial(pipeline_kernel, sections, parts, groups),
@@ -211,6 +348,8 @@
             pltpu.VMEM((blocks, side, width), jnp.bfloat16),
             pltpu.VMEM((blocks, side, width), jnp.bfloat16),
             pltpu.VMEM((2, blocks, side, width), jnp.bfloat16),
+            pltpu.VMEM((relayed, side, width), jnp.bfloat16),
+            pltpu.VMEM((relayed, side, width), jnp.bfloat16),
             dma,
             dma((2, groups)),
             dma((2, groups)),
@@ -218,21 +357,23 @@
             dma((blocks,)),
             dma((2, blocks)),
             dma((2, blocks)),
-        ],
+        ] + [dma((relayed,))] * 6,
         compiler_params=pltpu.CompilerParams(
             collective_id=0, has_side_effects=True, vmem_limit_bytes=56 * 2**20
         ),
     )(table, group_order[0], layer_inputs.reshape(blocks, side, width), adjacency, weights[0])
 
     placed = pl.pallas_call(
-        place_kernel,
+        functools.partial(place_kernel, groups),
         out_shape=jax.ShapeDtypeStruct((blocks, side, width), jnp.bfloat16),
-        grid_spec=pltpu.PrefetchScalarGridSpec(
-            num_scalar_prefetch=1,
-            grid=(groups,),
-            in_specs=[pl.BlockSpec((bg, side, width), lambda k, o: (k, 0, 0))],
-            out_specs=pl.BlockSpec((bg, side, width), lambda k, o: (o[k], 0, 0)),
-        ),
+        in_specs=[
+            pl.BlockSpec(memory_space=pltpu.SMEM),
+            pl.BlockSpec(memory_space=pl.ANY),
+        ],
+        out_specs=pl.BlockSpec(memory_space=pl.ANY),
+        scratch_shapes=[
+            pltpu.VMEM((blocks, side, width), jnp.bfloat16), dma((groups,)), dma((groups,)),
+        ],
     )(group_order[0], hidden)
     return placed.reshape(1, rows, width)
 

time: 160 us -> 151 us (0.944)
  Pallas kernels: 151 us -> 142 us
    pallas_call x1, Pallas kernels: 147 us -> 139 us  [on_device(): pl.pallas_call(functools.partial(pipeline_kernel, sections, parts, groups...]
where the time goes in v2:
time: 151 us; the launch traced here: 150 us
  Pallas kernels  142 us (94%)
  other arithmetic  3.11 us (2%)
  waiting for transfers between devices  2.55 us (2%)
  starting transfers between devices  1.77 us (1%)
    pallas_call x1, Pallas kernels, on_device(): pl.pallas_call(functools.partial(pipeline_kernel, sections, parts, groups...  139 us
    pallas_call x1, Pallas kernels, on_device(): pl.pallas_call(functools.partial(place_kernel, groups), out_shape=jax.Sha...  3.09 us
  transfers between devices with their start and end apart: 2, of which 1 were waited for; matrix products, arithmetic and copies ran while one was open for 1% of the time, Pallas kernels for 0%

profile of v2, /device:TPU:27, one launch (start us, length us, event | category | flops | bytes accessed | tf_op | source)
XLA Modules:
  0.0 150.4 jit_solution(9991740402051572154)
XLA Ops:
  0.0 1.8 %collective-permute-start = (s32[1,4]{1,0:T(1,128)}, s32[1,4]{1,0:T(1,128)S(1)}, u32[]{:S(2)}, u32[]{:S(2)}) collective-permute-start(s32[1,4]{1,0:T(1,128)} %param.8), channel_id=1, source_target_pairs={{0,1},{1,2},{2,3},{3,4},{4,5},{5,6},{6,7},{7,0},{8,9},{9,10},{10,1... | collective-permute-start | bytes 56 | tf_op jit(solution)/shard_map/ppermute | solution.py:311
  1.8 0.0 collective-permute-start.1
  1.8 0.8 iota_compare_fusion.2
  2.5 0.7 fusion.3
  3.2 0.0 collective-permute-done
  3.3 2.5 %collective-permute-done.1 = s32[1,4]{1,0:T(1,128)S(1)} collective-permute-done((s32[1,4]{1,0:T(1,128)}, s32[1,4]{1,0:T(1,128)S(1)}, u32[]{:S(2)}, u32[]{:S(2)}) %collective-permute-start.1) | collective-permute-done | bytes 48 | tf_op jit(solution)/shard_map/ppermute | solution.py:312
  5.8 0.7 pad_add_fusion
  6.5 0.1 select_reduce_fusion.2
  6.6 0.1 broadcast_in_dim.67
  6.6 0.1 broadcast_in_dim.70
  6.7 0.1 le.10
  6.8 0.1 select_reduce_fusion
  6.9 0.7 fusion.5
  7.6 0.1 copy.10
  7.7 0.1 select_reduce_fusion.1
  7.8 0.6 reshape.38.table
  8.4 138.9 %shard_map.55.h_hbm = bf16[16,128,512]{2,1,0:T(8,128)(2,1)} custom-call(s32[128]{0:T(128)} %reshape.38.table, s32[4]{0:T(128)} %bitcast.11, bf16[16,128,512]{2,1,0:T(8,128)(2,1)} %bitcast.7, bf16[16,8,128,128]{3,2,1,0:T(8,128)(2,1)} %adj_hbm.1, bf16[512,512]{1,0:T(8,128)(2,1)} %bitcast.8), custom_call_target="tpu_custom_call" | custom-call | tf_op jit(solution)/shard_map/pallas_call | solution.py:334
  147.3 3.1 %shard_map.56 = bf16[16,128,512]{2,1,0:T(8,128)(2,1)} custom-call(s32[4]{0:T(128)} %bitcast.12, bf16[16,128,512]{2,1,0:T(8,128)(2,1)} %shard_map.55.h_hbm), custom_call_target="tpu_custom_call" | custom-call | tf_op jit(solution)/shard_map/pallas_call | solution.py:366
  (1 shorter events, 0.0 us)
Async XLA Ops:
  0.0 3.2 %collective-permute-start = (s32[1,4]{1,0:T(1,128)}, s32[1,4]{1,0:T(1,128)S(1)}, u32[]{:S(2)}, u32[]{:S(2)}) collective-permute-start(s32[1,4]{1,0:T(1,128)} %param.8), channel_id=1, source_target_pairs={{0,1},{1,2},{2,3},{3,4},{4,5},{5,6},{6,7},{7,0},{8,9},{9,10},{10,1... | collective-permute-start | bytes 56 | tf_op jit(solution)/shard_map/ppermute | solution.py:311
  1.8 4.0 %collective-permute-start.1 = (s32[1,4]{1,0:T(1,128)}, s32[1,4]{1,0:T(1,128)S(1)}, u32[]{:S(2)}, u32[]{:S(2)}) collective-permute-start(s32[1,4]{1,0:T(1,128)} %param.8), channel_id=1, source_target_pairs={{1,0},{2,1},{3,2},{4,3},{5,4},{6,5},{7,6},{0,7},{9,8},{10,9},{11,1... | collective-permute-start | bytes 56 | tf_op jit(solution)/shard_map/ppermute | solution.py:312

commit v3 on v2

--- a/solution.py
+++ b/solution.py
@@ -16,7 +16,8 @@
 
 
 def pipeline_kernel(
-    sections, parts, groups, table, order, x_ref, adj_hbm, w_ref, out_ref,
+    sections, parts, groups, columns, own_order, order_ref, x_ref, adj_hbm, w_ref, out_ref,
+    table, position, order_land, near_order, order_send, order_recv, order_local,
     adj, src, mine, own_land, side_land, relay_up, relay_over,
     adj_sem, stale_send, stale_recv, z_send, z_recv, f_send, f_recv,
     up_send, up_recv, over_send, over_recv, down_send, down_recv,
@@ -40,7 +41,7 @@
     load_adj.start()
 
     for k in range(groups):
-        piece = x_ref[pl.ds(order[k] * bg, bg)]
+        piece = x_ref[pl.ds(own_order[0, k] * bg, bg)]
         mine[k * bg:(k + 1) * bg] = piece
         src[blocks + k * bg:blocks + (k + 1) * bg] = piece
 
@@ -69,6 +70,19 @@
             pl.semaphore_signal(barrier, inc=1, device_id={"section": 0}, device_id_type=MESH)
 
     pl.semaphore_wait(barrier, peers)
+
+    def order_copy(way):
+        return pltpu.make_async_remote_copy(
+            src_ref=order_ref,
+            dst_ref=order_land.at[way],
+            send_sem=order_send.at[way],
+            recv_sem=order_recv.at[way],
+            device_id={"dom": right if way == 0 else left},
+            device_id_type=MESH,
+        )
+
+    for way in range(2):
+        order_copy(way).start()
 
     def stale_copy(way, k):
         base = (0 if way == 0 else 2 * blocks) + k * bg
@@ -188,6 +202,36 @@
             for way in range(2):
                 stale_copy(way, k).start()
 
+    for way in range(2):
+        order_copy(way).wait()
+        local = pltpu.make_async_copy(
+            order_land.at[way], near_order.at[way], order_local.at[way]
+        )
+        local.start()
+        local.wait()
+
+    for p in range(3):
+        for g in range(groups):
+            step = jnp.int32(0)
+            for k in range(1, groups):
+                held = own_order[0, k] if p == 1 else near_order[p // 2, 0, k]
+                step = jnp.where(held == g, k, step)
+            position[p * groups + g] = step
+
+    later = s > 0
+
+    @pl.loop(0, blocks)
+    def _(r):
+        k = r // bg
+        row = own_order[0, k] * bg + r % bg
+        for t in range(tiles):
+            column = columns[row, t]
+            relative = jnp.minimum(lax.rem(lax.div(column, blocks) - d + 1 + parts, parts), 2)
+            inside = lax.rem(column, blocks)
+            step = position[relative * groups + lax.div(inside, bg)]
+            slot = relative * blocks + step * bg + lax.rem(inside, bg)
+            table[r * tiles + t] = slot + jnp.where(later & (step <= k), fresh, 0)
+
     load_adj.wait()
     own_base = jnp.where(s > 0, fresh + blocks, blocks)
 
@@ -230,7 +274,7 @@
 
         @pl.loop(lo, hi)
         def _(r):
-            row = order[k] * bg + (r - lo)
+            row = own_order[0, k] * bg + (r - lo)
             a = jnp.concatenate([adj[row, t] for t in range(tiles)], axis=1)
             h = jnp.concatenate([src[table[r * tiles + t]] for t in range(tiles)], axis=0)
             agg = jnp.dot(a, h, preferred_element_type=jnp.float32).astype(jnp.bfloat16)
@@ -300,35 +344,9 @@
 
 def on_device(sections, layer_inputs, adjacency, columns, group_order, weights):
     parts = lax.axis_size("dom")
-    d = lax.axis_index("dom")
-    s = lax.axis_index("section")
     rows, width = layer_inputs.shape[1:]
     blocks, tiles, side = adjacency.shape[:3]
     groups = group_order.shape[1]
-    bg = blocks // groups
-    up = [(i, (i + 1) % parts) for i in range(parts)]
-    down = [(j, i) for i, j in up]
-    before = lax.ppermute(group_order, "dom", up)
-    after = lax.ppermute(group_order, "dom", down)
-    orders = jnp.concatenate([before, group_order, after], axis=0)
-    ids = jnp.arange(groups, dtype=jnp.int32)
-    position = jnp.sum(
-        jnp.where(orders[:, :, None] == ids[None, None, :], ids[None, :, None], 0), axis=1
-    ).astype(jnp.int32)
-    relative = (columns // blocks - d + 1) % parts
-    inside = columns % blocks
-    key = relative * groups + inside // bg
-    flat = position.reshape(-1)
-    hits = key[:, :, None] == jnp.arange(3 * groups, dtype=jnp.int32)[None, None, :]
-    tile_pos = jnp.sum(jnp.where(hits, flat[None, None, :], 0), axis=2)
-    row_pos = jnp.repeat(position[1], bg)
-    is_fresh = (tile_pos <= row_pos[:, None]) & (s > 0)
-    slot = relative * blocks + tile_pos * bg + inside % bg + jnp.where(is_fresh, 3 * blocks, 0)
-    by_pos = slot.reshape(groups, bg, tiles)
-    pick = group_order[0][:, None] == ids[None, :]
-    table = jnp.sum(jnp.where(pick[:, :, None, None], by_pos[None], 0), axis=1)
-    table = table.reshape(-1).astype(jnp.int32)
-
     relayed = sum(count for _, _, count in relay_plan(sections, blocks))
     dma = pltpu.SemaphoreType.DMA
     hidden = pl.pallas_call(
@@ -338,11 +356,19 @@
             pl.BlockSpec(memory_space=pltpu.SMEM),
             pl.BlockSpec(memory_space=pltpu.SMEM),
             pl.BlockSpec(memory_space=pltpu.VMEM),
+            pl.BlockSpec(memory_space=pltpu.VMEM),
             pl.BlockSpec(memory_space=pl.ANY),
             pl.BlockSpec(memory_space=pltpu.VMEM),
         ],
         out_specs=pl.BlockSpec(memory_space=pltpu.VMEM),
         scratch_shapes=[
+            pltpu.SMEM((blocks * tiles,), jnp.int32),
+            pltpu.SMEM((3 * groups,), jnp.int32),
+            pltpu.VMEM((2, 1, groups), jnp.int32),
+            pltpu.SMEM((2, 1, groups), jnp.int32),
+            dma((2,)),
+            dma((2,)),
+            dma((2,)),
             pltpu.VMEM(adjacency.shape, jnp.bfloat16),
             pltpu.VMEM((6 * blocks, side, width), jnp.bfloat16),
             pltpu.VMEM((blocks, side, width), jnp.bfloat16),
@@ -361,7 +387,10 @@
         compiler_params=pltpu.CompilerParams(
             collective_id=0, has_side_effects=True, vmem_limit_bytes=56 * 2**20
         ),
-    )(table, group_order[0], layer_inputs.reshape(blocks, side, width), adjacency, weights[0])
+    )(
+        columns, group_order, group_order,
+        layer_inputs.reshape(blocks, side, width), adjacency, weights[0],
+    )
 
     placed = pl.pallas_call(
         functools.partial(place_kernel, groups),

time: 151 us -> 147 us (0.974)
  other arithmetic: 3.11 us -> 0 us
  Pallas kernels: 142 us -> 145 us
  waiting for transfers between devices: 2.55 us -> 0 us
  starting transfers between devices: 1.77 us -> 0 us
    pallas_call x1, Pallas kernels: 139 us -> 142 us  [on_device(): pl.pallas_call(functools.partial(pipeline_kernel, sections, parts, groups...]
    ppermute x2 -> x0, waiting for transfers between devices: 2.55 us -> none  [the longest x1 2.55 us: on_device(): after = lax.ppermute(group_order, 'dom', down)]
    ppermute x2 -> x0, starting transfers between devices: 1.77 us -> none  [the longest x1 1.77 us: on_device(): before = lax.ppermute(group_order, 'dom', up)]
  transfers between devices with their start and end apart: 2 -> 0, of which waited for: 1 -> 0; matrix products, arithmetic and copies ran while one was open for 1% -> 0% of each run, Pallas kernels for 0% -> 0%
where the time goes in v3:
time: 147 us
  Pallas kernels  145 us (99%)
    pallas_call x1, Pallas kernels, on_device(): pl.pallas_call(functools.partial(pipeline_kernel, sections, parts, groups...  142 us
    pallas_call x1, Pallas kernels, on_device(): pl.pallas_call(functools.partial(place_kernel, groups), out_shape=jax.Sha...  3.09 us

profile of v3, /device:TPU:27, one launch (start us, length us, event | category | flops | bytes accessed | tf_op | source)
XLA Modules:
  0.0 146.6 jit_solution(2718524871521950288)
XLA Ops:
  0.0 1.4 copy.6.columns
  1.4 142.1 %shard_map.55.h_hbm = bf16[16,128,512]{2,1,0:T(8,128)(2,1)} custom-call(s32[16,8]{1,0:T(8,128)} %copy.6.columns, s32[1,4]{1,0:T(1,128)} %order_ref.1, s32[1,4]{1,0:T(1,128)} %order_ref.1, bf16[16,128,512]{2,1,0:T(8,128)(2,1)} %bitcast.4, bf16[16,8,128,128]{3,2,1,0:T(8,128)(2,1)} %adj_hbm.1, bf16[512,512]{1,0:T(8,128)(2,1)} %bitcast.5), custom_call_target="tpu_custom_call" | custom-call | tf_op jit(solution)/shard_map/pallas_call | solution.py:352
  143.5 3.1 %shard_map.56 = bf16[16,128,512]{2,1,0:T(8,128)(2,1)} custom-call(s32[4]{0:T(128)} %bitcast.6, bf16[16,128,512]{2,1,0:T(8,128)(2,1)} %shard_map.55.h_hbm), custom_call_target="tpu_custom_call" | custom-call | tf_op jit(solution)/shard_map/pallas_call | solution.py:395

commit v4 on v3

--- a/solution.py
+++ b/solution.py
@@ -165,6 +165,11 @@
             device_id_type=MESH,
         )
 
+    def forward(r):
+        up_copy(r).wait_recv()
+        side_copy(0, r).start()
+        side_copy(1, r).start()
+
     @pl.when(s == 0)
     def _():
         across_copy().start()
@@ -240,11 +245,10 @@
 
         @pl.when(s > 0)
         def _():
-            @pl.loop(lo, hi)
-            def _(r):
-                up_copy(r).wait_recv()
-                side_copy(0, r).start()
-                side_copy(1, r).start()
+            if k == 0:
+                @pl.loop(lo, hi)
+                def _(r):
+                    forward(r)
 
             src[fresh + blocks + lo:fresh + blocks + hi] = own_land[lo:hi]
 
@@ -274,6 +278,11 @@
 
         @pl.loop(lo, hi)
         def _(r):
+            if k + 1 < groups:
+                @pl.when(s > 0)
+                def _():
+                    forward(r + bg)
+
             row = own_order[0, k] * bg + (r - lo)
             a = jnp.concatenate([adj[row, t] for t in range(tiles)], axis=1)
             h = jnp.concatenate([src[table[r * tiles + t]] for t in range(tiles)], axis=0)

time: 147 us -> 142 us (0.966)
  Pallas kernels: 145 us -> 139 us
    pallas_call x1, Pallas kernels: 142 us -> 136 us  [on_device(): pl.pallas_call(functools.partial(pipeline_kernel, sections, parts, groups...]
where the time goes in v4:
time: 142 us; the launch traced here: 141 us
  Pallas kernels  139 us (98%)
    pallas_call x1, Pallas kernels, on_device(): pl.pallas_call(functools.partial(pipeline_kernel, sections, parts, groups...  136 us
    pallas_call x1, Pallas kernels, on_device(): pl.pallas_call(functools.partial(place_kernel, groups), out_shape=jax.Sha...  3.09 us

profile of v4, /device:TPU:27, one launch (start us, length us, event | category | flops | bytes accessed | tf_op | source)
XLA Modules:
  0.0 140.6 jit_solution(17162469724565724654)
XLA Ops:
  0.0 1.4 copy.6.columns
  1.4 136.1 %shard_map.55.h_hbm = bf16[16,128,512]{2,1,0:T(8,128)(2,1)} custom-call(s32[16,8]{1,0:T(8,128)} %copy.6.columns, s32[1,4]{1,0:T(1,128)} %order_ref.1, s32[1,4]{1,0:T(1,128)} %order_ref.1, bf16[16,128,512]{2,1,0:T(8,128)(2,1)} %bitcast.4, bf16[16,8,128,128]{3,2,1,0:T(8,128)(2,1)} %adj_hbm.1, bf16[512,512]{1,0:T(8,128)(2,1)} %bitcast.5), custom_call_target="tpu_custom_call" | custom-call | tf_op jit(solution)/shard_map/pallas_call | solution.py:361
  137.5 3.1 %shard_map.56 = bf16[16,128,512]{2,1,0:T(8,128)(2,1)} custom-call(s32[4]{0:T(128)} %bitcast.6, bf16[16,128,512]{2,1,0:T(8,128)(2,1)} %shard_map.55.h_hbm), custom_call_target="tpu_custom_call" | custom-call | tf_op jit(solution)/shard_map/pallas_call | solution.py:404
